TPU v7x, 32 devices: a whole 2x2x4 slice. The times are simulated.
32 devices in a mesh: row: 4 (over y, x), col: 4 (over z), depth: 2 (over core).
Axes of the slice: x: 2, y: 2, z: 4, core: 2. Of those that a mesh axis runs over, the one named last changes fastest.
Arguments:
- orbitals: bfloat16 [2, 1024, 2, 4096], P(None, ('row', 'col'), 'depth'), may hold values from -20 to 20
- potential: float32 [2, 4096], P('depth'), may hold values from -6 to 6
Outputs:
- intersection: float32 [1024, 2, 1024], P(('row', 'depth'), None, 'col')
- applied: bfloat16 [2, 1024, 2, 4096], P(None, ('row', 'col'), 'depth')
All inputs are finite; a program needn't handle non-finite values.
Results may differ from a plain program's by a relative error of at most 0.001.
Values may be sent and summed in bfloat16 or wider, within the bound.
A program may use at most 128 MiB of HBM per device.

v0:
```python
import jax
import jax.numpy as jnp
from jax import lax
from jax.sharding import PartitionSpec as P

NX = 64


def with_halo(block, sides, width):
    for axis, dim in sides:
        count = lax.axis_size(axis)
        forward = [(i, i + 1) for i in range(count - 1)]
        forward.append((count - 1, 0))
        backward = [(target, source) for source, target in forward]
        low = lax.ppermute(
            lax.slice_in_dim(block, block.shape[dim] - width, None, axis=dim), axis, forward
        )
        high = lax.ppermute(lax.slice_in_dim(block, 0, width, axis=dim), axis, backward)
        block = jnp.concatenate([low, block, high], axis=dim)
    return block


def apply_operator(padded, potential):
    center = padded[:, :, 1:-1].astype(jnp.float32)
    below = padded[:, :, :-2].astype(jnp.float32)
    above = padded[:, :, 2:].astype(jnp.float32)
    flat_cells = center.shape[-1]
    xpos = jnp.arange(flat_cells) % NX
    yminus = jnp.roll(center, NX, axis=3)
    yplus = jnp.roll(center, -NX, axis=3)
    xminus = jnp.where(xpos == 0, jnp.roll(center, 1 - NX, axis=3), jnp.roll(center, 1, axis=3))
    xplus = jnp.where(
        xpos == NX - 1, jnp.roll(center, NX - 1, axis=3), jnp.roll(center, -1, axis=3)
    )
    lap = below + above + yminus + yplus + xminus + xplus - 6.0 * center
    return (-0.5 * lap + potential[None, None] * center).astype(jnp.bfloat16)


def contract(left, right):
    return lax.dot_general(
        left, right, (((1,), (1,)), ((), ())), preferred_element_type=jnp.float32
    )


def shards(orbitals, potential):
    parts, orbs, planes, cells = orbitals.shape
    flat = orbitals.reshape(parts, orbs, planes * cells)
    panel = lax.all_gather(flat, "col", axis=1, tiled=True)
    other = lax.all_gather(flat, "row", axis=1, tiled=True)
    padded = with_halo(orbitals, (("depth", 2),), 1)
    applied = apply_operator(padded, potential)
    dvol = 1.0 / (planes * lax.axis_size("depth") * cells)
    tile_cols = other.shape[1]
    real_rows = panel[0]
    imag_rows = panel[1]
    sreal = contract(real_rows, other[0]) + contract(imag_rows, other[1])
    simag = contract(real_rows, other[1]) - contract(imag_rows, other[0])
    summed = lax.psum_scatter(
        dvol * jnp.concatenate([sreal, simag], axis=1), "depth", scatter_dimension=0, tiled=True
    )
    intersection = summed.reshape(summed.shape[0], 2, tile_cols)
    intersection = lax.all_to_all(intersection, "col", split_axis=2, concat_axis=2, tiled=True)
    return (intersection, applied)


def solution(mesh):
    in_specs = (P(None, ("row", "col"), "depth", None), P("depth", None))
    out_specs = (P(("row", "depth"), None, "col"), P(None, ("row", "col"), "depth", None))
    return jax.shard_map(shards, mesh=mesh, in_specs=in_specs, out_specs=out_specs, check_vma=False)
```

profile of v0, /device:TPU:0, one launch (start us, length us, event | category | flops | bytes accessed | tf_op | source)
XLA Modules:
  0.0 186.1 jit_solution(16060242905263434024)
XLA Ops:
  7.2 0.0 copy-start
  7.2 0.0 all-gather.7.cloned.1.call-start
  7.2 0.7 all-gather.7.cloned.1.call-update
  7.9 0.0 all-gather.5.cloned.1.call-start
  8.0 0.7 all-gather.5.cloned.1.call-update
  8.7 0.0 reduce-scatter.2.cloned.1.call-start
  8.7 0.0 copy-done
  8.7 0.6 collective-permute-start
  9.3 0.1 collective-permute-start.1
  9.4 0.1 fusion.23
  9.4 0.7 fusion.20
  10.1 0.7 fusion.19
  10.8 1.8 fusion.21
  12.7 2.4 %fusion.22 = (f32[2,64,1,4032]{3,1,2,0:T(8,128)}, f32[2,64,1,4032]{3,1,2,0:T(8,128)}) fusion(bf16[2,64,1,4096]{3,1,2,0:T(8,128)(2,1)S(1)} %copy-done), kind=kLoop, calls=%fused_computation.32 | loop fusion | bytes 8257536 | tf_op jit(solution)/shard_map/jit(_roll_static)/slice | solution.py:30
  15.1 50.1 %all-gather.7.cloned.1.call-done = bf16[2,256,1,4096]{3,1,2,0:T(8,128)(2,1)} async-done(((bf16[2,64,1,4096]{3,1,2,0:T(8,128)(2,1)}), bf16[2,256,1,4096]{3,1,2,0:T(8,128)(2,1)}) %all-gather.7.cloned.1.call-update) | async-done | bytes 4194320 | tf_op jit(solution)/shard_map/all_gather | solution.py:49
  65.2 82.3 %all-gather.5.cloned.1.call-done = bf16[2,256,1,4096]{3,1,2,0:T(8,128)(2,1)} async-done(((bf16[2,64,1,4096]{3,1,2,0:T(8,128)(2,1)}), bf16[2,256,1,4096]{3,1,2,0:T(8,128)(2,1)}) %all-gather.5.cloned.1.call-update) | async-done | bytes 4194320 | tf_op jit(solution)/shard_map/all_gather | solution.py:48
  147.5 0.0 copy-start.2
  147.5 3.1 %fusion.7 = f32[256,256]{0,1:T(8,128)S(1)} fusion(bf16[2,256,1,4096]{3,1,2,0:T(8,128)(2,1)} %all-gather.5.cloned.1.call-done, bf16[2,256,1,4096]{3,1,2,0:T(8,128)(2,1)} %all-gather.7.cloned.1.call-done), kind=kOutput, calls=%fused_computation.14 | convolution fusion | flops 536870912 | bytes 4456448 | tf_op jit(solution)/shard_map/dot_general | solution.py:40
  150.6 0.3 copy-done.2
  150.9 0.0 copy-start.3
  150.9 2.5 %fusion.8 = f32[256,256]{0,1:T(8,128)S(1)} fusion(bf16[2,256,1,4096]{3,1,2,0:T(8,128)(2,1)} %all-gather.5.cloned.1.call-done, bf16[2,256,1,4096]{3,1,2,0:T(8,128)(2,1)S(1)} %copy-done.2), kind=kOutput, calls=%fused_computation.15 | convolution fusion | flops 536870912 | bytes 4456448 | tf_op jit(solution)/shard_map/dot_general | solution.py:40
  153.4 0.3 copy-done.3
  153.8 0.7 fusion.12
  154.5 0.7 fusion.11
  155.3 0.8 maximum_multiply_fusion
  156.1 0.0 reduce-scatter.2.cloned.1.call-update
  156.1 0.6 fusion.15
  156.7 0.0 copy-start.1
  156.7 2.4 %fusion.18 = (f32[2,64,1,4095]{3,1,2,0:T(8,128)}, f32[2,64,1,4095]{3,1,2,0:T(8,128)}) fusion(bf16[2,64,1,4096]{3,1,2,0:T(8,128)(2,1)S(1)} %copy-done), kind=kLoop, calls=%fused_computation.28 | loop fusion | bytes 8386560 | tf_op jit(solution)/shard_map/jit(_roll_static)/slice | solution.py:33
  159.1 3.5 %reduce-scatter.2.cloned.1.call-done = f32[128,512]{0,1:T(8,128)} async-done(((f32[256,512]{0,1:T(8,128)}), f32[128,512]{0,1:T(8,128)}) %reduce-scatter.2.cloned.1.call-update) | async-done | bytes 262160 | tf_op jit(solution)/shard_map/reduce_scatter | solution.py:58
  162.7 1.9 copy.7
  164.5 4.8 %all-to-all-start = ((f32[128,2,256]{0,1,2:T(2,128)}), f32[128,2,256]{0,1,2:T(2,128)S(1)}, u32[]{:S(2)}, u32[]{:S(2)}) async-start(f32[128,2,256]{0,1,2:T(2,128)} %copy.7), calls=%async_computation.1 | async-start | bytes 524288 | tf_op jit(solution)/shard_map/all_to_all | solution.py:62
  169.3 0.0 collective-permute-done
  169.3 0.0 collective-permute-done.1
  169.3 0.0 copy-done.1
  169.3 6.8 %fusion.6 = bf16[2,64,1,4096]{3,1,2,0:T(8,128)(2,1)} fusion(f32[2,64,1,4032]{3,1,2,0:T(8,128)} %get-tuple-element.15, f32[2,64,1,64]{3,1,2,0:T(8,128)S(1)} %get-tuple-element.17, f32[2,64,1,64]{3,1,2,0:T(8,128)S(1)} %get-tuple-element.16, f32[2,64,1,4032]{3,1,2,0:T(8,128)} %get-tuple-element.14, f32[2,64,1,63]{3,1,2,0:T(8,128)} %get-tuple-element.11, ...), kind=kLoop, calls=%fused_computation.11 | loop fusion | flops 11534336 | bytes 16801792 | tf_op jit(solution)/shard_map/convert_element_type | solution.py:36
  176.2 2.6 %all-to-all-done = f32[128,2,256]{0,1,2:T(2,128)S(1)} async-done(((f32[128,2,256]{0,1,2:T(2,128)}), f32[128,2,256]{0,1,2:T(2,128)S(1)}, u32[]{:S(2)}, u32[]{:S(2)}) %all-to-all-start) | async-done | bytes 262176 | tf_op jit(solution)/shard_map/all_to_all | solution.py:62
  178.7 0.8 copy.8
Async XLA Ops:
  7.2 1.5 copy-start
  7.2 58.0 %all-gather.7.cloned.1.call-start = ((), (), s32[]{:S(2)}) async-start(), calls=%async_computation.4 | async-start | bytes 5242880 | tf_op jit(solution)/shard_map/all_gather | solution.py:49
  7.9 139.6 %all-gather.5.cloned.1.call-start = ((), (), s32[]{:S(2)}) async-start(), calls=%async_computation.3 | async-start | bytes 5242880 | tf_op jit(solution)/shard_map/all_gather | solution.py:48
  8.7 154.0 %reduce-scatter.2.cloned.1.call-start = ((), (), s32[]{:S(2)}) async-start(), calls=%async_computation.2 | async-start | bytes 786432 | tf_op jit(solution)/shard_map/reduce_scatter | solution.py:58
  8.7 160.6 %collective-permute-start = (bf16[2,64,1,4096]{3,1,2,0:T(8,128)(2,1)S(1)}, bf16[2,64,1,4096]{3,1,2,0:T(8,128)(2,1)}, u32[]{:S(2)}, u32[]{:S(2)}) collective-permute-start(bf16[2,64,1,4096]{3,1,2,0:T(8,128)(2,1)S(1)} %copy-done), channel_id=1, source_target_pairs={{0,1},{1,0},{2,3},{3,2},{4,5},{5,4},{6,7},{7,6},{8,9},{9,8},{10,11... | collective-permute-start | bytes 3145736 | tf_op jit(solution)/shard_map/ppermute | solution.py:15
  9.3 160.1 %collective-permute-start.1 = (bf16[2,64,1,4096]{3,1,2,0:T(8,128)(2,1)S(1)}, bf16[2,64,1,4096]{3,1,2,0:T(8,128)(2,1)}, u32[]{:S(2)}, u32[]{:S(2)}) collective-permute-start(bf16[2,64,1,4096]{3,1,2,0:T(8,128)(2,1)S(1)} %copy-done), channel_id=1, source_target_pairs={{1,0},{0,1},{3,2},{2,3},{5,4},{4,5},{7,6},{6,7},{9,8},{8,9},{11,10... | collective-permute-start | bytes 3145736 | tf_op jit(solution)/shard_map/ppermute | solution.py:18
  147.5 3.4 %copy-start.2 = (bf16[2,256,1,4096]{3,1,2,0:T(8,128)(2,1)S(1)}, bf16[2,256,1,4096]{3,1,2,0:T(8,128)(2,1)}, u32[]{:S(2)}) copy-start(bf16[2,256,1,4096]{3,1,2,0:T(8,128)(2,1)} %all-gather.7.cloned.1.call-done) | copy-start | bytes 12582916
  150.9 2.8 %copy-start.3 = (bf16[2,256,1,4096]{3,1,2,0:T(8,128)(2,1)S(1)}, bf16[2,256,1,4096]{3,1,2,0:T(8,128)(2,1)}, u32[]{:S(2)}) copy-start(bf16[2,256,1,4096]{3,1,2,0:T(8,128)(2,1)} %all-gather.5.cloned.1.call-done) | copy-start | bytes 12582916
  156.7 12.6 %copy-start.1 = (f32[1,4096]{1,0:T(1,128)S(1)}, f32[1,4096]{1,0:T(1,128)}, u32[]{:S(2)}) copy-start(f32[1,4096]{1,0:T(1,128)} %param.3) | copy-start | bytes 49156
  164.5 14.2 %all-to-all-start = ((f32[128,2,256]{0,1,2:T(2,128)}), f32[128,2,256]{0,1,2:T(2,128)S(1)}, u32[]{:S(2)}, u32[]{:S(2)}) async-start(f32[128,2,256]{0,1,2:T(2,128)} %copy.7), calls=%async_computation.1 | async-start | bytes 524288 | tf_op jit(solution)/shard_map/all_to_all | solution.py:62
Sparse Core Ops, SparseCore 0:
  9.8 55.2 all-gather.6
  66.7 80.7 all-gather.4
  156.2 6.3 reduce-scatter.1
where the time goes:
time: 186 us
  waiting for transfers between devices  140 us (75%)
  between operations  13.8 us (7%)
  local copies, waits for them, and re-layouts  11.5 us (6%)
  other arithmetic  8.25 us (4%)
  matrix products  7.07 us (4%)
  starting transfers between devices  5.54 us (3%)
    all_gather x1, waiting for transfers between devices, shards(): panel = lax.all_gather(flat, 'col', axis=1, tiled=True)  82.3 us
    all_gather x1, waiting for transfers between devices, shards(): other = lax.all_gather(flat, 'row', axis=1, tiled=True)  50.1 us
    dot_general x4, matrix products, contract(): lax.dot_general(left, right, (((1,), (1,)), ((), ())), preferred_element_...  7.07 us
    convert_element_type x1, other arithmetic, apply_operator(): return (-0.5 * lap + potential[None, None] * center).astype(jnp.bfloat16)  6.81 us
    all_to_all x1, starting transfers between devices, shards(): lax.all_to_all(intersection, 'col', split_axis=2, concat_axis=2, tiled=True)  4.79 us
  transfers between devices with their start and end apart: 6, of which 4 were waited for; matrix products, arithmetic and copies ran while one was open for 14% of the time, Pallas kernels for 0%

commit v1 on v0

--- a/solution.py
+++ b/solution.py
@@ -4,6 +4,25 @@
 from jax.sharding import PartitionSpec as P
 
 NX = 64
+
+
+def pack_stages_all_in(axis_name, array_in):
+    total_devices = jax.lax.psum(1, axis_name=axis_name)
+    blocks_here = [array_in]
+    for jj in range(total_devices - 1):
+        blocks_here.append(
+            jax.lax.ppermute(
+                blocks_here[-1],
+                axis_name,
+                [(t, (t + 1) % total_devices) for t in range(total_devices)],
+            )
+        )
+    current_block = jnp.roll(
+        jnp.concatenate(blocks_here[::-1], 1),
+        (jax.lax.axis_index(axis_name) + 1) * array_in.shape[1],
+        1,
+    )
+    return current_block
 
 
 def with_halo(block, sides, width):
@@ -46,7 +65,7 @@
     parts, orbs, planes, cells = orbitals.shape
     flat = orbitals.reshape(parts, orbs, planes * cells)
     panel = lax.all_gather(flat, "col", axis=1, tiled=True)
-    other = lax.all_gather(flat, "row", axis=1, tiled=True)
+    other = pack_stages_all_in("row", flat)
     padded = with_halo(orbitals, (("depth", 2),), 1)
     applied = apply_operator(padded, potential)
     dvol = 1.0 / (planes * lax.axis_size("depth") * cells)

time: 186 us -> 144 us (0.77)
  waiting for transfers between devices: 140 us -> 75 us
  local copies, waits for them, and re-layouts: 11.5 us -> 27.2 us
  starting transfers between devices: 5.54 us -> 9.28 us
  matrix products: 7.07 us -> 10.1 us
    all_gather x1, waiting for transfers between devices: 82.3 us -> 0.01 us  [shards(): panel = lax.all_gather(flat, 'col', axis=1, tiled=True)]
    ppermute x0 -> x3, waiting for transfers between devices: none -> 67.4 us  [pack_stages_all_in(): jax.lax.ppermute(blocks_here[-1], axis_name, [(t, (t + 1) % total_devices...]
    all_gather x1 -> x0, waiting for transfers between devices: 50.1 us -> none  [shards(): other = lax.all_gather(flat, 'row', axis=1, tiled=True)]
    unnamed x9 -> x14, local copies, waits for them, and re-layouts: 1.52 us -> 15.9 us
    ppermute x0 -> x3, starting transfers between devices: none -> 3.8 us  [pack_stages_all_in(): jax.lax.ppermute(blocks_here[-1], axis_name, [(t, (t + 1) % total_devices...]
    dot_general x4, matrix products: 7.07 us -> 10.1 us  [contract(): lax.dot_general(left, right, (((1,), (1,)), ((), ())), preferred_element_...]
  transfers between devices with their start and end apart: 6 -> 8, of which waited for: 4 -> 5; matrix products, arithmetic and copies ran while one was open for 14% -> 31% of each run, Pallas kernels for 0% -> 0%
where the time goes in v1:
time: 144 us
  waiting for transfers between devices  75 us (52%)
  local copies, waits for them, and re-layouts  27.2 us (19%)
  between operations  14.1 us (10%)
  matrix products  10.1 us (7%)
  starting transfers between devices  9.28 us (6%)
  other arithmetic  8.25 us (6%)
    ppermute x3, waiting for transfers between devices, pack_stages_all_in(): jax.lax.ppermute(blocks_here[-1], axis_name, [(t, (t + 1) % total_devices...  67.4 us
    unnamed x14, local copies, waits for them, and re-layouts  15.9 us
    dot_general x4, matrix products, contract(): lax.dot_general(left, right, (((1,), (1,)), ((), ())), preferred_element_...  10.1 us
    convert_element_type x1, other arithmetic, apply_operator(): return (-0.5 * lap + potential[None, None] * center).astype(jnp.bfloat16)  6.81 us
    reduce_scatter x1, waiting for transfers between devices, shards(): lax.psum_scatter(dvol * jnp.concatenate([sreal, simag], axis=1), 'depth',...  4.99 us
    all_to_all x1, starting transfers between devices, shards(): lax.all_to_all(intersection, 'col', split_axis=2, concat_axis=2, tiled=True)  4.83 us
    ppermute x3, starting transfers between devices, pack_stages_all_in(): jax.lax.ppermute(blocks_here[-1], axis_name, [(t, (t + 1) % total_devices...  3.8 us
    slice x2, local copies, waits for them, and re-layouts, apply_operator(): yplus = jnp.roll(center, -NX, axis=3)  3.18 us
  transfers between devices with their start and end apart: 8, of which 5 were waited for; matrix products, arithmetic and copies ran while one was open for 31% of the time, Pallas kernels for 0%

profile of v1, /device:TPU:0, one launch (start us, length us, event | category | flops | bytes accessed | tf_op | source)
XLA Modules:
  0.0 143.9 jit_solution(1244582738047880500)
XLA Ops:
  7.2 0.0 copy-start
  7.2 0.0 all-gather.3.cloned.1.call-start
  7.2 3.0 %collective-permute-start = (bf16[2,64,4096]{2,1,0:T(8,128)(2,1)}, bf16[2,64,4096]{2,1,0:T(8,128)(2,1)}, u32[]{:S(2)}, u32[]{:S(2)}) collective-permute-start(bf16[2,64,4096]{2,1,0:T(8,128)(2,1)} %bitcast.41), channel_id=1, source_target_pairs={{0,8},{8,16},{16,24},{24,0},{1,9},{9,17},{17,25},{25,1},{2,10},{10... | collective-permute-start | bytes 3145736 | tf_op jit(solution)/shard_map/ppermute | solution.py:14
  10.2 0.0 all-gather.3.cloned.1.call-update
  10.3 0.0 reduce-scatter.2.cloned.1.call-start
  10.3 0.1 collective-permute-start.3
  10.4 0.5 collective-permute-start.4
  10.9 23.8 %collective-permute-done = bf16[2,64,4096]{2,1,0:T(8,128)(2,1)} collective-permute-done((bf16[2,64,4096]{2,1,0:T(8,128)(2,1)}, bf16[2,64,4096]{2,1,0:T(8,128)(2,1)}, u32[]{:S(2)}, u32[]{:S(2)}) %collective-permute-start) | collective-permute-done | bytes 1048608 | tf_op jit(solution)/shard_map/ppermute | solution.py:14
  34.7 0.8 collective-permute-start.1
  35.5 0.0 copy-done
  35.5 1.8 %fusion.27 = (f32[2,64,1,4033]{3,1,2,0:T(8,128)S(1)}, f32[2,64,1,4033]{3,1,2,0:T(8,128)}) fusion(bf16[2,64,1,4096]{3,1,2,0:T(8,128)(2,1)S(1)} %copy-done), kind=kLoop, calls=%fused_computation.45 | loop fusion | bytes 8259584 | tf_op jit(solution)/shard_map/jit(_roll_static)/slice | solution.py:52
  37.3 0.1 fusion.26
  37.4 0.7 fusion.29
  38.1 22.1 %collective-permute-done.1 = bf16[2,64,4096]{2,1,0:T(8,128)(2,1)} collective-permute-done((bf16[2,64,4096]{2,1,0:T(8,128)(2,1)}, bf16[2,64,4096]{2,1,0:T(8,128)(2,1)}, u32[]{:S(2)}, u32[]{:S(2)}) %collective-permute-start.1) | collective-permute-done | bytes 1048608 | tf_op jit(solution)/shard_map/ppermute | solution.py:14
  60.2 0.0 collective-permute-start.2
  60.2 0.7 fusion.25
  60.9 2.5 %fusion.28 = (f32[2,64,1,4032]{3,1,2,0:T(8,128)}, f32[2,64,1,4032]{3,1,2,0:T(8,128)}) fusion(bf16[2,64,1,4096]{3,1,2,0:T(8,128)(2,1)S(1)} %copy-done), kind=kLoop, calls=%fused_computation.46 | loop fusion | bytes 8257536 | tf_op jit(solution)/shard_map/jit(_roll_static)/slice | solution.py:49
  63.4 21.5 %collective-permute-done.2 = bf16[2,64,4096]{2,1,0:T(8,128)(2,1)} collective-permute-done((bf16[2,64,4096]{2,1,0:T(8,128)(2,1)}, bf16[2,64,4096]{2,1,0:T(8,128)(2,1)}, u32[]{:S(2)}, u32[]{:S(2)}) %collective-permute-start.2) | collective-permute-done | bytes 1048608 | tf_op jit(solution)/shard_map/ppermute | solution.py:14
  84.9 2.3 %constant_dynamic-update-slice_fusion.7 = bf16[2,512,4096]{2,1,0:T(8,128)(2,1)} fusion(bf16[2,64,4096]{2,1,0:T(8,128)(2,1)} %collective-permute-done.2), kind=kLoop, calls=%fused_computation.31 | loop fusion | bytes 2097152
  87.2 2.3 %constant_dynamic-update-slice_fusion.6 = bf16[2,512,4096]{2,1,0:T(8,128)(2,1)} fusion(bf16[2,512,4096]{2,1,0:T(8,128)(2,1)} %constant_dynamic-update-slice_fusion.7, bf16[2,64,4096]{2,1,0:T(8,128)(2,1)} %collective-permute-done.1), kind=kLoop, calls=%fused_computation.30 | loop fusion | bytes 2097152
  89.5 2.3 %constant_dynamic-update-slice_fusion.5 = bf16[2,512,4096]{2,1,0:T(8,128)(2,1)} fusion(bf16[2,512,4096]{2,1,0:T(8,128)(2,1)} %constant_dynamic-update-slice_fusion.6, bf16[2,64,4096]{2,1,0:T(8,128)(2,1)} %collective-permute-done), kind=kLoop, calls=%fused_computation.29 | loop fusion | bytes 2097152
  91.7 1.1 constant_dynamic-update-slice_fusion.4
  92.8 2.3 %constant_dynamic-update-slice_fusion.3 = bf16[2,512,4096]{2,1,0:T(8,128)(2,1)} fusion(bf16[2,512,4096]{2,1,0:T(8,128)(2,1)} %constant_dynamic-update-slice_fusion.4, bf16[2,64,4096]{2,1,0:T(8,128)(2,1)} %collective-permute-done.2), kind=kLoop, calls=%fused_computation.27 | loop fusion | bytes 2097152
  95.1 2.3 %constant_dynamic-update-slice_fusion.2 = bf16[2,512,4096]{2,1,0:T(8,128)(2,1)} fusion(bf16[2,512,4096]{2,1,0:T(8,128)(2,1)} %constant_dynamic-update-slice_fusion.3, bf16[2,64,4096]{2,1,0:T(8,128)(2,1)} %collective-permute-done.1), kind=kLoop, calls=%fused_computation.26 | loop fusion | bytes 2097152
  97.4 2.3 %constant_dynamic-update-slice_fusion.1 = bf16[2,512,4096]{2,1,0:T(8,128)(2,1)} fusion(bf16[2,512,4096]{2,1,0:T(8,128)(2,1)} %constant_dynamic-update-slice_fusion.2, bf16[2,64,4096]{2,1,0:T(8,128)(2,1)} %collective-permute-done), kind=kLoop, calls=%fused_computation.25 | loop fusion | bytes 2097152
  99.7 1.1 constant_dynamic-update-slice_fusion
  100.8 0.0 all-gather.3.cloned.1.call-done
  100.8 0.0 copy-start.2
  100.8 3.1 %fusion.9 = f32[256,256]{1,0:T(8,128)S(1)} fusion(bf16[2,256,1,4096]{3,1,2,0:T(8,128)(2,1)} %all-gather.3.cloned.1.call-done, bf16[2,512,4096]{2,1,0:T(8,128)(2,1)} %constant_dynamic-update-slice_fusion, s32[]{:T(128)S(6)} %select_n.45), kind=kOutput, calls=%fused_computation.16 | convolution fusion | flops 536870912 | bytes 4456452 | tf_op jit(solution)/shard_map/dot_general | solution.py:59
  103.9 0.3 copy-done.2
  104.2 2.3 %fusion.10 = f32[256,256]{1,0:T(8,128)S(1)} fusion(bf16[2,256,1,4096]{3,1,2,0:T(8,128)(2,1)S(1)} %copy-done.2, bf16[2,512,4096]{2,1,0:T(8,128)(2,1)} %constant_dynamic-update-slice_fusion, s32[]{:T(128)S(6)} %add.59, s32[]{:T(128)S(6)} %select_n.45), kind=kOutput, calls=%fused_computation.17 | convolution fusion | flops 536870912 | bytes 4456456 | tf_op jit(solution)/shard_map/dot_general | solution.py:59
  106.6 2.3 %fusion.12 = f32[256,256]{0,1:T(8,128)S(1)} fusion(f32[256,256]{1,0:T(8,128)S(1)} %fusion.10, bf16[2,256,1,4096]{3,1,2,0:T(8,128)(2,1)S(1)} %copy-done.2, bf16[2,512,4096]{2,1,0:T(8,128)(2,1)} %constant_dynamic-update-slice_fusion, s32[]{:T(128)S(6)} %select_n.45), kind=kOutput, calls=%fused_computation.19 | convolution fusion | flops 536936448 | bytes 4718596 | tf_op jit(solution)/shard_map/dot_general | solution.py:59
  108.9 2.3 %fusion.14 = f32[256,256]{0,1:T(8,128)S(1)} fusion(f32[256,256]{1,0:T(8,128)S(1)} %fusion.9, bf16[2,256,1,4096]{3,1,2,0:T(8,128)(2,1)S(1)} %copy-done.2, bf16[2,512,4096]{2,1,0:T(8,128)(2,1)} %constant_dynamic-update-slice_fusion, s32[]{:T(128)S(6)} %add.59, s32[]{:T(128)S(6)} %select_n.45), kind=kOutput, calls=%fused_computation.21 | convolution fusion | flops 536936448 | bytes 4718600 | tf_op jit(solution)/shard_map/dot_general | solution.py:59
  111.3 0.8 maximum_multiply_fusion
  112.1 0.0 reduce-scatter.2.cloned.1.call-update
  112.1 0.6 fusion.17
  112.7 0.0 copy-start.1
  112.7 2.4 %fusion.24 = (f32[2,64,1,4095]{3,1,2,0:T(8,128)}, f32[2,64,1,4095]{3,1,2,0:T(8,128)}) fusion(bf16[2,64,1,4096]{3,1,2,0:T(8,128)(2,1)S(1)} %copy-done), kind=kLoop, calls=%fused_computation.42 | loop fusion | bytes 8386560 | tf_op jit(solution)/shard_map/jit(_roll_static)/slice | solution.py:52
  115.2 5.0 %reduce-scatter.2.cloned.1.call-done = f32[128,512]{0,1:T(8,128)} async-done(((f32[256,512]{0,1:T(8,128)}), f32[128,512]{0,1:T(8,128)}) %reduce-scatter.2.cloned.1.call-update) | async-done | bytes 262160 | tf_op jit(solution)/shard_map/reduce_scatter | solution.py:77
  120.2 1.9 %copy.7 = f32[128,2,256]{0,1,2:T(2,128)} copy(f32[128,2,256]{0,2,1:T(8,128)} %bitcast.42) | data formatting | bytes 524288 | tf_op jit(solution)/shard_map/reshape | solution.py:80
  122.0 4.8 %all-to-all-start = ((f32[128,2,256]{0,1,2:T(2,128)}), f32[128,2,256]{0,1,2:T(2,128)S(1)}, u32[]{:S(2)}, u32[]{:S(2)}) async-start(f32[128,2,256]{0,1,2:T(2,128)} %copy.7), calls=%async_computation.1 | async-start | bytes 524288 | tf_op jit(solution)/shard_map/all_to_all | solution.py:81
  126.8 0.0 collective-permute-done.3
  126.8 0.0 collective-permute-done.4
  126.9 0.0 copy-done.1
  126.9 6.8 %fusion.6 = bf16[2,64,1,4096]{3,1,2,0:T(8,128)(2,1)} fusion(f32[2,64,1,4032]{3,1,2,0:T(8,128)} %get-tuple-element.15, f32[2,64,1,64]{3,1,2,0:T(8,128)} %get-tuple-element.17, f32[2,64,1,64]{3,1,2,0:T(8,128)} %get-tuple-element.16, f32[2,64,1,4032]{3,1,2,0:T(8,128)} %get-tuple-element.14, f32[2,64,1,63]{3,1,2,0:T(8,128)S(1)} %get-tuple-element.11, ...), kind=kLoop, calls=%fused_computation.11 | loop fusion | flops 11534336 | bytes 16801792 | tf_op jit(solution)/shard_map/convert_element_type | solution.py:55
  133.7 2.6 %all-to-all-done = f32[128,2,256]{0,1,2:T(2,128)S(1)} async-done(((f32[128,2,256]{0,1,2:T(2,128)}), f32[128,2,256]{0,1,2:T(2,128)S(1)}, u32[]{:S(2)}, u32[]{:S(2)}) %all-to-all-start) | async-done | bytes 262176 | tf_op jit(solution)/shard_map/all_to_all | solution.py:81
  136.2 0.8 copy.8
Async XLA Ops:
  7.2 28.3 %copy-start = (bf16[2,64,1,4096]{3,1,2,0:T(8,128)(2,1)S(1)}, bf16[2,64,1,4096]{3,1,2,0:T(8,128)(2,1)}, u32[]{:S(2)}) copy-start(bf16[2,64,1,4096]{3,1,2,0:T(8,128)(2,1)} %param.2) | copy-start | bytes 3145732
  7.2 93.6 %all-gather.3.cloned.1.call-start = ((), (), s32[]{:S(2)}) async-start(), calls=%async_computation.3 | async-start | bytes 5242880 | tf_op jit(solution)/shard_map/all_gather | solution.py:67
  7.2 27.5 %collective-permute-start = (bf16[2,64,4096]{2,1,0:T(8,128)(2,1)}, bf16[2,64,4096]{2,1,0:T(8,128)(2,1)}, u32[]{:S(2)}, u32[]{:S(2)}) collective-permute-start(bf16[2,64,4096]{2,1,0:T(8,128)(2,1)} %bitcast.41), channel_id=1, source_target_pairs={{0,8},{8,16},{16,24},{24,0},{1,9},{9,17},{17,25},{25,1},{2,10},{10... | collective-permute-start | bytes 3145736 | tf_op jit(solution)/shard_map/ppermute | solution.py:14
  10.3 109.9 %reduce-scatter.2.cloned.1.call-start = ((), (), s32[]{:S(2)}) async-start(), calls=%async_computation.2 | async-start | bytes 786432 | tf_op jit(solution)/shard_map/reduce_scatter | solution.py:77
  10.3 116.5 %collective-permute-start.3 = (bf16[2,64,1,4096]{3,1,2,0:T(8,128)(2,1)}, bf16[2,64,1,4096]{3,1,2,0:T(8,128)(2,1)}, u32[]{:S(2)}, u32[]{:S(2)}) collective-permute-start(bf16[2,64,1,4096]{3,1,2,0:T(8,128)(2,1)} %param.2), channel_id=1, source_target_pairs={{0,1},{1,0},{2,3},{3,2},{4,5},{5,4},{6,7},{7,6},{8,9},{9,8},{10,11... | collective-permute-start | bytes 3145736 | tf_op jit(solution)/shard_map/ppermute | solution.py:34
  10.4 116.5 %collective-permute-start.4 = (bf16[2,64,1,4096]{3,1,2,0:T(8,128)(2,1)}, bf16[2,64,1,4096]{3,1,2,0:T(8,128)(2,1)}, u32[]{:S(2)}, u32[]{:S(2)}) collective-permute-start(bf16[2,64,1,4096]{3,1,2,0:T(8,128)(2,1)} %param.2), channel_id=1, source_target_pairs={{1,0},{0,1},{3,2},{2,3},{5,4},{4,5},{7,6},{6,7},{9,8},{8,9},{11,10... | collective-permute-start | bytes 3145736 | tf_op jit(solution)/shard_map/ppermute | solution.py:37
  34.7 25.5 %collective-permute-start.1 = (bf16[2,64,4096]{2,1,0:T(8,128)(2,1)}, bf16[2,64,4096]{2,1,0:T(8,128)(2,1)}, u32[]{:S(2)}, u32[]{:S(2)}) collective-permute-start(bf16[2,64,4096]{2,1,0:T(8,128)(2,1)} %collective-permute-done), channel_id=1, source_target_pairs={{0,8},{8,16},{16,24},{24,0},{1,9},{9,17},{17,25},{25,1},{2,10},{10... | collective-permute-start | bytes 3145736 | tf_op jit(solution)/shard_map/ppermute | solution.py:14
  60.2 24.7 %collective-permute-start.2 = (bf16[2,64,4096]{2,1,0:T(8,128)(2,1)}, bf16[2,64,4096]{2,1,0:T(8,128)(2,1)}, u32[]{:S(2)}, u32[]{:S(2)}) collective-permute-start(bf16[2,64,4096]{2,1,0:T(8,128)(2,1)} %collective-permute-done.1), channel_id=1, source_target_pairs={{0,8},{8,16},{16,24},{24,0},{1,9},{9,17},{17,25},{25,1},{2,10},{10... | collective-permute-start | bytes 3145736 | tf_op jit(solution)/shard_map/ppermute | solution.py:14
  100.8 3.4 %copy-start.2 = (bf16[2,256,1,4096]{3,1,2,0:T(8,128)(2,1)S(1)}, bf16[2,256,1,4096]{3,1,2,0:T(8,128)(2,1)}, u32[]{:S(2)}) copy-start(bf16[2,256,1,4096]{3,1,2,0:T(8,128)(2,1)} %all-gather.3.cloned.1.call-done) | copy-start | bytes 12582916
  112.7 14.1 %copy-start.1 = (f32[1,4096]{1,0:T(1,128)S(1)}, f32[1,4096]{1,0:T(1,128)}, u32[]{:S(2)}) copy-start(f32[1,4096]{1,0:T(1,128)} %param.3) | copy-start | bytes 49156
  122.0 14.2 %all-to-all-start = ((f32[128,2,256]{0,1,2:T(2,128)}), f32[128,2,256]{0,1,2:T(2,128)S(1)}, u32[]{:S(2)}, u32[]{:S(2)}) async-start(f32[128,2,256]{0,1,2:T(2,128)} %copy.7), calls=%async_computation.1 | async-start | bytes 524288 | tf_op jit(solution)/shard_map/all_to_all | solution.py:81
Sparse Core Ops, SparseCore 0:
  10.4 82.6 all-gather.2
  112.3 7.8 reduce-scatter.1
